TPU v7x, 32 devices: a whole 2x2x4 slice. The times are simulated.
32 devices in a mesh: section: 2 (over x), lat: 4 (over z), lon: 4 (over y, core).
Axes of the slice: x: 2, y: 2, z: 4, core: 2. Of those that a mesh axis runs over, the one named last changes fastest.
Arguments:
- state: bfloat16 [2, 112, 360, 1024], P('section', 'lat', 'lon'), may hold values from -6 to 6
- fresh: bfloat16 [112, 360, 1024], P('lat', 'lon'), may hold values from -6 to 6
- cutoff: int32 [3], replicated, may hold values from 0 to 15
- plan: int32 [2, 2], replicated, may hold values from 0 to 1
- lmax: int32 [2], replicated, may hold values from 56 to 112, as said below
- mmax: int32 [2], replicated, may hold values from 24 to 96, as said below
- cutoff_table: float32 [16, 1024], replicated, may hold values from -3 to 3
- norm_gains: float32 [2, 2, 2, 1024], P('section'), may hold values from 0.1 to 1.9
- filters: float32 [2, 2, 2, 112, 1024], P('section', None, None, None, 'lon'), may hold values from -5 to 5
- w_in: bfloat16 [2, 2, 1024, 4096], P('section', None, 'lat'), may hold values from -0.1875 to 0.1875
- w_out: bfloat16 [2, 2, 1024, 4096], P('section', None, 'lat'), may hold values from -0.09375 to 0.09375
Outputs:
- first_pass: bfloat16 [2, 112, 360, 1024], P('section', 'lat', 'lon')
- second_pass: bfloat16 [2, 112, 360, 1024], P('section', 'lat', 'lon')
Inputs may be any that keep to these rules, and one draw needn't show every extreme that they name: `lmax`: some section keeps all 112 degrees in every draw. `mmax`: some section keeps all 96 wavenumbers in every draw.
All inputs are finite; a program needn't handle non-finite values.
Results may differ from a plain program's by a relative error of at most 0.01.
Values may be sent and summed in bfloat16 or wider, within the bound.
No kernel may reach another device: no remote copies, remote signals or barrier semaphores. Data moves between devices by JAX's collectives and lax.ppermute only.
A program may use at most 384 MiB of HBM per device.

v0:
```python
import math
import jax
import jax.numpy as jnp
from jax import lax
from jax.sharding import PartitionSpec as P

MM = 96


def passed_along(value, axis, steps):
    count = lax.axis_size(axis)
    leading, last = (max(0, -steps), min(count, count - steps))
    return lax.ppermute(value, axis, [(source, source + steps) for source in range(leading, last)])


def legendre_table(orders, n_rows, n_degrees):
    rows = jnp.arange(n_rows, dtype=jnp.float32)
    theta = math.pi * (rows + 0.5) / n_rows
    cosine = jnp.cos(theta)
    sine = jnp.sin(theta)
    order = orders[:, None]
    log_start = (
        0.5 * jnp.log((2.0 * order + 1.0) / (4.0 * math.pi))
        + jax.scipy.special.gammaln(order + 0.5)
        - jax.scipy.special.gammaln(0.5)
        - jax.scipy.special.gammaln(order + 1.0)
        + order * jnp.log(sine)[None, :]
    )
    start = jnp.exp(log_start)

    def advance(carry, degree):
        last, before = carry
        level = degree.astype(jnp.float32)
        coef_a = jnp.sqrt(
            jnp.maximum(4.0 * level * level - 1.0, 1.0)
            / jnp.maximum(level * level - order * order, 1.0)
        )
        coef_b = jnp.sqrt(
            jnp.maximum((level - 1.0) ** 2 - order * order, 0.0)
            / jnp.maximum(4.0 * (level - 1.0) ** 2 - 1.0, 1.0)
        )
        general = coef_a * (cosine[None, :] * last - coef_b * before)
        fresh_row = jnp.where(
            level < order, jnp.zeros_like(start), jnp.where(level == order, start, general)
        )
        return ((fresh_row, last), fresh_row)

    _, table = lax.scan(
        advance,
        (jnp.zeros_like(start), jnp.zeros_like(start)),
        jnp.arange(n_degrees, dtype=jnp.int32),
    )
    quad = 2.0 * math.pi * (math.pi / n_rows) * sine
    return (table, table * quad[None, None, :])


def fourier_tables(n_lon):
    columns = jnp.arange(n_lon, dtype=jnp.int32)
    orders = jnp.arange(MM, dtype=jnp.int32)
    phase = 2.0 * math.pi * (columns[:, None] * orders[None, :] % n_lon).astype(jnp.float32) / n_lon
    cos_fwd = jnp.cos(phase) / n_lon
    sin_fwd = -jnp.sin(phase) / n_lon
    weight = jnp.where(orders == 0, 1.0, 2.0).astype(jnp.float32)[:, None]
    inverse = jnp.stack([weight * jnp.cos(phase).T, -weight * jnp.sin(phase).T], 0)
    return (cos_fwd, sin_fwd, inverse)


def layer_norm(values, gain):
    center = values - jnp.mean(values, axis=-1, keepdims=True)
    spread = jnp.mean(center * center, axis=-1, keepdims=True)
    return center * lax.rsqrt(spread + 1e-05) * gain


def pick(stack, index):
    return lax.dynamic_index_in_dim(stack, index, 0, keepdims=False)


def local(state, fresh, cutoff, plan, lmax, mmax, cutoff_table, norm_gains, filters, w_in, w_out):
    highest = lax.Precision.HIGHEST
    section_idx = lax.axis_index("section")
    lat_idx = lax.axis_index("lat")
    n_section = lax.axis_size("section")
    n_lat = lax.axis_size("lat")
    n_lon = lax.axis_size("lon")
    n_rows, n_cols, width = fresh.shape
    n_degrees = filters.shape[3]
    all_rows = n_rows * n_lat
    all_cols = n_cols * n_lon
    m_local = MM // n_lat
    m_global = lat_idx * m_local + jnp.arange(m_local, dtype=jnp.int32)
    plain, weighted = legendre_table(m_global.astype(jnp.float32), all_rows, n_degrees)
    cos_fwd, sin_fwd, inverse = fourier_tables(all_cols)
    l_max = pick(lmax, section_idx)
    m_max = pick(mmax, section_idx)
    keep = (
        (jnp.arange(n_degrees, dtype=jnp.int32) < l_max)[:, None] & (m_global < m_max)[None, :]
    ).astype(jnp.float32)[:, :, None]

    def run_block(tokens, tick):
        block_idx = pick(plan[tick], section_idx)
        cut = pick(cutoff, tick - section_idx + n_section - 1)
        gains = pick(norm_gains[0], block_idx)
        filt = pick(filters[0], block_idx)
        weight_in = pick(w_in[0], block_idx)
        weight_out = pick(w_out[0], block_idx)
        onehot = (jnp.arange(cutoff_table.shape[0], dtype=jnp.int32) == cut).astype(jnp.float32)
        embed = jnp.dot(onehot, cutoff_table, precision=highest)
        base = tokens.astype(jnp.float32) + embed
        normed = layer_norm(base, gains[0]).astype(jnp.bfloat16)
        by_lon = lax.all_to_all(normed, "lon", split_axis=2, concat_axis=1, tiled=True)
        wide = by_lon.astype(jnp.float32)
        real_part = jnp.einsum("jkc,km->jmc", wide, cos_fwd, precision=highest)
        imag_part = jnp.einsum("jkc,km->jmc", wide, sin_fwd, precision=highest)
        spectrum = jnp.stack([real_part, imag_part], 1).astype(jnp.bfloat16)
        by_mode = lax.all_to_all(spectrum, "lat", split_axis=2, concat_axis=0, tiled=True)
        coeff = jnp.einsum(
            "lmj,jrmc->rlmc", weighted, by_mode.astype(jnp.float32), precision=highest
        )
        filt_re = filt[0][:, None, :]
        filt_im = filt[1][:, None, :]
        out_re = keep * (coeff[0] * filt_re - coeff[1] * filt_im)
        out_im = keep * (coeff[0] * filt_im + coeff[1] * filt_re)
        synthesis = jnp.einsum(
            "lmj,rlmc->jrmc", plain, jnp.stack([out_re, out_im], 0), precision=highest
        ).astype(jnp.bfloat16)
        by_row = lax.all_to_all(synthesis, "lat", split_axis=0, concat_axis=2, tiled=True)
        spectral = jnp.einsum(
            "jrmc,rmk->jkc", by_row.astype(jnp.float32), inverse, precision=highest
        ).astype(jnp.bfloat16)
        spectral = lax.all_to_all(spectral, "lon", split_axis=1, concat_axis=2, tiled=True)
        mixed = base + spectral.astype(jnp.float32)
        normed_two = layer_norm(mixed, gains[1]).astype(jnp.bfloat16)
        flat = normed_two.reshape(n_rows * n_cols, width)
        before_act = jnp.dot(
            flat,
            lax.all_gather(weight_in, "lat", axis=0, tiled=True),
            preferred_element_type=jnp.float32,
        )
        hidden = jax.nn.gelu(before_act).astype(jnp.bfloat16)
        projected = lax.dot_general(
            hidden,
            lax.all_gather(weight_out, "lat", axis=0, tiled=True),
            (((1,), (1,)), ((), ())),
            preferred_element_type=jnp.float32,
        )
        result = mixed + projected.reshape(mixed.shape)
        return result.astype(jnp.bfloat16)

    first_out = run_block(state[0], 0)
    handed = passed_along(first_out, "section", 1)
    entering = jnp.where(section_idx == 0, fresh, handed)
    second_out = run_block(entering, 1)
    return (first_out[None], second_out[None])


def solution(mesh):
    return jax.shard_map(
        local,
        mesh=mesh,
        in_specs=(
            P("section", "lat", "lon", None),
            P("lat", "lon", None),
            P(),
            P(),
            P(),
            P(),
            P(),
            P("section", None, None, None),
            P("section", None, None, None, "lon"),
            P("section", None, "lat", None),
            P("section", None, "lat", None),
        ),
        out_specs=(P("section", "lat", "lon", None), P("section", "lat", "lon", None)),
        check_vma=False,
    )
```

profile of v0, /device:TPU:0, one launch (start us, length us, event | category | flops | bytes accessed | tf_op | source)
XLA Modules:
  0.0 1451.1 jit_solution(14158678115372856451)
XLA Ops:
  21.4 7.0 multiply_convert_fusion.2
  28.4 12.0 copy.147
  40.4 5.6 all-to-all-start
  46.7 4.7 constant_dynamic-slice_fusion.3
  51.6 88.3 %all-to-all-done = bf16[28,90,1024]{1,0,2:T(8,128)(2,1)} async-done(((bf16[28,90,1024]{1,0,2:T(8,128)(2,1)}), bf16[28,90,1024]{1,0,2:T(8,128)(2,1)}, u32[]{:S(2)}, u32[]{:S(2)}) %all-to-all-start) | async-done | bytes 5160992 | tf_op jit(solution)/shard_map/all_to_all | solution.py:110
  139.9 14.5 copy.148
  154.3 8.3 all_to_all.95
  162.6 6.3 fusion.72
  173.1 4.4 copy.149
  177.4 6.0 all-to-all-start.1
  183.4 162.5 %while.20 = (s32[]{:T(128)}, f32[24,112]{1,0:T(8,128)S(1)}, f32[24,112]{1,0:T(8,128)S(1)}, f32[112,24,112]{2,1,0:T(8,128)S(1)}, s32[112]{0:T(128)S(1)}, /*index=...) while((s32[]{:T(128)}, f32[24,112]{1,0:T(8,128)S(1)}, ...), condition=%wide.region_3.4_spmd.clone.clone.clone, body=%wide.region_2.3_spmd.clone.clone.clone.sunk | while | flops 24742 | bytes 66539 | solution.py:48
  354.5 3.9 fusion.62
  359.3 5.2 convert_bitcast_fusion.1
  368.2 5.1 all-to-all-start.2
  373.5 4.7 constant_dynamic-slice_fusion.2
  379.5 128.0 %all-to-all-done.2 = bf16[112,2,24,256]{3,1,2,0:T(2,128)(2,1)S(1)} async-done(((bf16[112,2,24,256]{3,1,2,0:T(2,128)(2,1)}), bf16[112,2,24,256]{3,1,2,0:T(2,128)(2,1)S(1)}, u32[]{:S(2)}, u32[]{:S(2)}) %all-to-all-start.2) | async-done | bytes 2752544 | tf_op jit(solution)/shard_map/all_to_all | solution.py:126
  508.3 4.6 fusion.47
  516.8 5.4 all-to-all-start.3
  522.2 8.2 reshape.641
  530.4 58.2 %all-to-all-done.3 = bf16[28,360,256]{2,0,1:T(8,128)(2,1)} async-done(((bf16[28,360,256]{2,0,1:T(8,128)(2,1)}), bf16[28,360,256]{2,0,1:T(8,128)(2,1)}, u32[]{:S(2)}, u32[]{:S(2)}) %all-to-all-start.3) | async-done | bytes 5160992 | tf_op jit(solution)/shard_map/all_to_all | solution.py:130
  588.6 9.5 copy_convert_fusion.1
  598.1 11.6 reshape.645
  609.7 14.5 copy.160
  624.2 14.0 reshape.643
  638.2 7.3 fusion.57
  645.5 8.0 multiply_reduce_fusion.2
  653.7 10.4 copy.191
  664.1 38.2 %fusion.16.clone.4 = bf16[2520,4096]{1,0:T(8,128)(2,1)} fusion(bf16[1,1,1024,4096]{3,2,1,0:T(8,128)(2,1)} %all-gather.9.cloned.1.call-done, f32[2520,1024]{1,0:T(8,128)} %bitcast.198, f32[2520,1024]{1,0:T(8,128)} %reshape.641, f32[1024]{0:T(1024)S(1)} %bitcast.218, f32[2520]{0:T(1024)S(1)} %rsqrt.37, f32[2520]{0:T(1024)S(1)} %div.110, ...), kind=kOutput, calls=%fused_computation.24.clone.clone.clone.1 | convolution fusion | flops 21247672320 | bytes 49704640 | tf_op jit(solution)/shard_map/dot_general | solution.py:134
  702.3 28.7 %fusion.34 = f32[2520,1024]{1,0:T(8,128)} fusion(bf16[1,1,1024,4096]{3,2,1,0:T(8,128)(2,1)} %all-gather.11.cloned.1.call-done, bf16[2520,4096]{1,0:T(8,128)(2,1)} %fusion.16.clone.4), kind=kOutput, calls=%fused_computation.56 | convolution fusion | flops 21139292160 | bytes 39354368 | tf_op jit(solution)/shard_map/dot_general | solution.py:140
  731.0 11.1 reshape.636
  742.0 12.8 add_convert_fusion.1
  754.8 5.8 collective-permute-start
  761.3 114.8 %collective-permute-done = bf16[28,90,1024]{2,1,0:T(8,128)(2,1)} collective-permute-done((bf16[28,90,1024]{2,1,0:T(8,128)(2,1)}, bf16[28,90,1024]{2,1,0:T(8,128)(2,1)}, u32[]{:S(2)}, u32[]{:S(2)}) %collective-permute-start) | collective-permute-done | bytes 5160992 | tf_op jit(solution)/shard_map/ppermute | solution.py:13
  876.1 4.6 fusion.27
  883.2 3.9 multiply_convert_fusion.1
  887.1 12.0 copy.163
  899.1 5.6 all-to-all-start.4
  905.5 92.4 %all-to-all-done.4 = bf16[28,90,1024]{1,0,2:T(8,128)(2,1)} async-done(((bf16[28,90,1024]{1,0,2:T(8,128)(2,1)}), bf16[28,90,1024]{1,0,2:T(8,128)(2,1)}, u32[]{:S(2)}, u32[]{:S(2)}) %all-to-all-start.4) | async-done | bytes 5160992 | tf_op jit(solution)/shard_map/all_to_all | solution.py:110
  997.9 14.9 %copy.164 = bf16[28,90,4,256]{3,1,2,0:T(8,128)(2,1)} copy(bf16[28,90,4,256]{1,0,3,2:T(8,128)(2,1)} %bitcast.41) | data formatting | bytes 10321920 | tf_op jit(solution)/shard_map/all_to_all | solution.py:110
  1012.7 8.3 all_to_all.108
  1021.0 6.3 fusion.74
  1034.3 80.7 %all_to_all.126 = bf16[28,2,96,256]{3,1,0,2:T(2,128)(2,1)S(1)} all-to-all(bf16[28,2,96,256]{3,1,0,2:T(2,128)(2,1)S(1)} %copy.165), channel_id=1, replica_groups=mesh['section'=2,'lat'=4,'lon'=4] {'lat'}, dimensions={2} | all-to-all | bytes 5505024 | tf_op jit(solution)/shard_map/all_to_all | solution.py:115
  1116.3 3.9 fusion.65
  1121.6 5.1 convert_bitcast_fusion
  1128.9 64.8 %all_to_all.127 = bf16[112,2,24,256]{3,1,2,0:T(2,128)(2,1)S(1)} all-to-all(bf16[112,2,24,256]{3,1,2,0:T(2,128)(2,1)S(1)} %copy.171), channel_id=1, replica_groups=mesh['section'=2,'lat'=4,'lon'=4] {'lat'}, dimensions={0} | all-to-all | bytes 5505024 | tf_op jit(solution)/shard_map/all_to_all | solution.py:126
  1194.7 4.6 fusion.48
  1199.3 3.9 copy.174
  1203.1 5.2 all-to-all-start.7
  1209.0 10.9 reshape.635
  1219.9 13.8 reshape.640
  1233.7 12.9 add_convert_fusion.2
  1246.6 28.2 %all-to-all-done.7 = bf16[28,360,256]{2,0,1:T(8,128)(2,1)} async-done(((bf16[28,360,256]{2,0,1:T(8,128)(2,1)}), bf16[28,360,256]{2,0,1:T(8,128)(2,1)}, u32[]{:S(2)}, u32[]{:S(2)}) %all-to-all-start.7) | async-done | bytes 5160992 | tf_op jit(solution)/shard_map/all_to_all | solution.py:130
  1274.9 9.6 copy_convert_fusion
  1284.5 11.7 reshape.648
  1296.2 14.5 %copy.176 = f32[28,90,4,256]{3,2,1,0:T(4,128)} copy(f32[28,90,4,256]{3,1,2,0:T(8,128)} %bitcast.187) | data formatting | bytes 20643840 | tf_op jit(solution)/shard_map/convert_element_type | solution.py:131
  1310.7 14.0 reshape.644
  1324.7 7.4 fusion.157
  1332.1 8.1 multiply_reduce_fusion
  1340.3 8.4 multiply_convert_fusion
  1348.7 7.9 reshape.637
  1356.6 35.3 %fusion.24.clone.4 = bf16[2520,4096]{1,0:T(8,128)(2,1)} fusion(bf16[2520,1024]{1,0:T(8,128)(2,1)} %reshape.637, bf16[1,1,1024,4096]{3,2,1,0:T(8,128)(2,1)} %all-gather.13.cloned.1.call-done), kind=kOutput, calls=%fused_computation.32.clone.clone.clone.1 | convolution fusion | flops 21232189440 | bytes 34193408 | tf_op jit(solution)/shard_map/dot_general | solution.py:134
  1391.9 28.8 %fusion.30 = f32[2520,1024]{1,0:T(8,128)} fusion(bf16[1,1,1024,4096]{3,2,1,0:T(8,128)(2,1)} %all-gather.15.cloned.1.call-done, bf16[2520,4096]{1,0:T(8,128)(2,1)} %fusion.24.clone.4), kind=kOutput, calls=%fused_computation.53 | convolution fusion | flops 21139292160 | bytes 39354368 | tf_op jit(solution)/shard_map/dot_general | solution.py:140
  1420.7 10.8 reshape.638
  1431.5 12.8 fusion.38
  (684 shorter events, 135.7 us)
Async XLA Ops:
  7.2 5.5 copy-start
  11.1 6.3 copy-start.2
  13.6 7.2 copy-start.22
  40.4 99.5 %all-to-all-start = ((bf16[28,90,1024]{1,0,2:T(8,128)(2,1)}), bf16[28,90,1024]{1,0,2:T(8,128)(2,1)}, u32[]{:S(2)}, u32[]{:S(2)}) async-start(bf16[28,90,1024]{1,0,2:T(8,128)(2,1)} %copy.147), calls=%async_computation | async-start | bytes 16777216 | tf_op jit(solution)/shard_map/all_to_all | solution.py:110
  46.0 618.1 %all-gather.9.cloned.1.call-start = ((), (), s32[]{:S(2)}) async-start(), calls=%async_computation.8 | async-start | bytes 10485760 | tf_op jit(solution)/shard_map/all_gather | solution.py:136
  162.6 6.3 copy-start.4
  173.1 172.8 %copy-start.23 = (s32[2]{0:T(128)S(1)}, s32[2]{0:T(128)}, u32[]{:S(2)}) copy-start(s32[2]{0:T(128)} %param.18) | copy-start | bytes 28
  173.1 173.5 %copy-start.24 = (s32[2]{0:T(128)S(1)}, s32[2]{0:T(128)}, u32[]{:S(2)}) copy-start(s32[2]{0:T(128)} %param.17) | copy-start | bytes 28
  177.4 171.6 %copy-start.17 = (f32[1,2,2,112,256]{4,3,2,1,0:T(8,128)S(1)}, f32[1,2,2,112,256]{4,3,2,1,0:T(8,128)}, u32[]{:S(2)}) copy-start(f32[1,2,2,112,256]{4,3,2,1,0:T(8,128)} %param.21) | copy-start | bytes 1376260
  177.4 173.9 %all-to-all-start.1 = ((bf16[28,2,96,256]{3,1,0,2:T(2,128)(2,1)}), bf16[28,2,96,256]{3,1,0,2:T(2,128)(2,1)}, u32[]{:S(2)}, u32[]{:S(2)}) async-start(bf16[28,2,96,256]{3,1,0,2:T(2,128)(2,1)} %copy.149), calls=%async_computation.1 | async-start | bytes 5505024 | tf_op jit(solution)/shard_map/all_to_all | solution.py:115
  345.9 3.9 copy-start.10
  347.7 11.6 copy-start.6
  349.9 8.5 copy-start.18
  351.3 3.2 copy-start.8
  368.2 139.3 %all-to-all-start.2 = ((bf16[112,2,24,256]{3,1,2,0:T(2,128)(2,1)}), bf16[112,2,24,256]{3,1,2,0:T(2,128)(2,1)S(1)}, u32[]{:S(2)}, u32[]{:S(2)}) async-start(bf16[112,2,24,256]{3,1,2,0:T(2,128)(2,1)} %copy.155), calls=%async_computation.2 | async-start | bytes 5505024 | tf_op jit(solution)/shard_map/all_to_all | solution.py:126
  373.3 329.0 %all-gather.11.cloned.1.call-start = ((), (), s32[]{:S(2)}) async-start(), calls=%async_computation.9 | async-start | bytes 10485760 | tf_op jit(solution)/shard_map/all_gather | solution.py:142
  378.9 129.4 %copy-start.11 = (f32[1,96,360]{2,1,0:T(8,128)}, f32[1,96,360]{2,1,0:T(8,128)S(1)}, u32[]{:S(2)}) copy-start(f32[1,96,360]{2,1,0:T(8,128)S(1)} %cosine_multiply_fusion.1) | copy-start | bytes 414724
  379.5 128.8 %copy-start.13 = (f32[1,96,360]{2,1,0:T(8,128)}, f32[1,96,360]{2,1,0:T(8,128)S(1)}, u32[]{:S(2)}) copy-start(f32[1,96,360]{2,1,0:T(8,128)S(1)} %sine_multiply_fusion) | copy-start | bytes 414724
  516.8 71.8 %all-to-all-start.3 = ((bf16[28,360,256]{2,0,1:T(8,128)(2,1)}), bf16[28,360,256]{2,0,1:T(8,128)(2,1)}, u32[]{:S(2)}, u32[]{:S(2)}) async-start(bf16[28,360,256]{2,0,1:T(8,128)(2,1)} %copy.158), calls=%async_computation.3 | async-start | bytes 11796480 | tf_op jit(solution)/shard_map/all_to_all | solution.py:130
  754.8 121.3 %collective-permute-start = (bf16[28,90,1024]{2,1,0:T(8,128)(2,1)}, bf16[28,90,1024]{2,1,0:T(8,128)(2,1)}, u32[]{:S(2)}, u32[]{:S(2)}) collective-permute-start(bf16[28,90,1024]{2,1,0:T(8,128)(2,1)} %add_convert_fusion.1), channel_id=1, source_target_pairs={{0,16},{1,17},{2,18},{3,19},{4,20},{5,21},{6,22},{7,23},{8,24},{9,... | collective-permute-start | bytes 15482888 | tf_op jit(solution)/shard_map/ppermute | solution.py:13
  880.7 2.5 copy-start.3
  880.8 2.4 copy-start.21
  899.1 98.8 %all-to-all-start.4 = ((bf16[28,90,1024]{1,0,2:T(8,128)(2,1)}), bf16[28,90,1024]{1,0,2:T(8,128)(2,1)}, u32[]{:S(2)}, u32[]{:S(2)}) async-start(bf16[28,90,1024]{1,0,2:T(8,128)(2,1)} %copy.163), calls=%async_computation.4 | async-start | bytes 16777216 | tf_op jit(solution)/shard_map/all_to_all | solution.py:110
  904.7 451.9 %all-gather.13.cloned.1.call-start = ((), (), s32[]{:S(2)}) async-start(), calls=%async_computation.10 | async-start | bytes 10485760 | tf_op jit(solution)/shard_map/all_gather | solution.py:136
  1021.0 6.3 copy-start.5
  1115.0 1.3 copy-start.9
  1115.9 4.3 copy-start.15
  1115.9 4.3 copy-start.16
  1115.9 4.3 copy-start.19
  1120.2 1.3 copy-start.7
  1193.7 0.9 copy-start.12
  1193.7 1.0 copy-start.14
  1203.1 71.7 %all-to-all-start.7 = ((bf16[28,360,256]{2,0,1:T(8,128)(2,1)}), bf16[28,360,256]{2,0,1:T(8,128)(2,1)}, u32[]{:S(2)}, u32[]{:S(2)}) async-start(bf16[28,360,256]{2,0,1:T(8,128)(2,1)} %copy.174), calls=%async_computation.7 | async-start | bytes 11796480 | tf_op jit(solution)/shard_map/all_to_all | solution.py:130
  1208.4 183.5 %all-gather.15.cloned.1.call-start = ((), (), s32[]{:S(2)}) async-start(), calls=%async_computation.11 | async-start | bytes 10485760 | tf_op jit(solution)/shard_map/all_gather | solution.py:142
  1324.7 15.6 %slice-start = ((s8[5505024]{0:T(1024)(128)(4,1)}), s8[4194304]{0:T(1024)(128)(4,1)S(1)}, s32[]{:S(2)}) async-start(s8[5505024]{0:T(1024)(128)(4,1)} %bitcast.183), calls=%async_computation.12 | async-start | bytes 8388608
  1332.1 8.2 slice-start.1
  1332.1 8.2 copy-start.20
  1431.5 12.8 copy-start.1
Sparse Core Ops, SparseCore 0:
  51.5 178.2 all-gather.8
  378.4 191.6 all-gather.10
  907.1 178.0 all-gather.12
  1210.5 149.1 all-gather.14
where the time goes:
time: 1460 us; the launch traced here: 1450 us
  waiting for transfers between devices  511 us (35%)
  local copies, waits for them, and re-layouts  333 us (23%)
  matrix products  180 us (12%)
  blocking collectives  146 us (10%)
  other arithmetic  145 us (10%)
  loops' own time  78.3 us (5%)
  starting transfers between devices  39.6 us (3%)
  between operations  18.6 us (1%)
    all_to_all x2, waiting for transfers between devices, run_block(): lax.all_to_all(normed, 'lon', split_axis=2, concat_axis=1, tiled=True)  181 us
    all_to_all x1, waiting for transfers between devices, run_block(): lax.all_to_all(synthesis, 'lat', split_axis=0, concat_axis=2, tiled=True)  128 us
    ppermute x1, waiting for transfers between devices, passed_along(): lax.ppermute(value, axis, [(source, source + steps) for source in range(l...  115 us
    convert_element_type x7, local copies, waits for them, and re-layouts, run_block(): mixed = base + spectral.astype(jnp.float32)  94 us
    all_to_all x2, waiting for transfers between devices, run_block(): lax.all_to_all(spectral, 'lon', split_axis=1, concat_axis=2, tiled=True)  86.5 us
    all_to_all x1, blocking collectives, run_block(): lax.all_to_all(spectrum, 'lat', split_axis=2, concat_axis=0, tiled=True)  80.7 us
    another operation x1, loops' own time, legendre_table(): lax.scan(advance, (jnp.zeros_like(start), jnp.zeros_like(start)), jnp.ara...  78.3 us
    dot_general x2, matrix products, run_block(): jnp.dot(flat, lax.all_gather(weight_in, 'lat', axis=0, tiled=True), prefe...  73.5 us
  transfers between devices with their start and end apart: 11, of which 6 were waited for; matrix products, arithmetic and copies ran while one was open for 33% of the time, Pallas kernels for 0%

commit v1 on v0

--- a/solution.py
+++ b/solution.py
@@ -127,7 +127,12 @@
         spectral = jnp.einsum(
             "jrmc,rmk->jkc", by_row.astype(jnp.float32), inverse, precision=highest
         ).astype(jnp.bfloat16)
-        spectral = lax.all_to_all(spectral, "lon", split_axis=1, concat_axis=2, tiled=True)
+        spectral = jnp.concatenate(
+            lax.all_to_all(
+                jnp.stack(jnp.split(spectral, lax.axis_size("lon"), axis=1)), "lon", 0, 0
+            ),
+            axis=2,
+        )
         mixed = base + spectral.astype(jnp.float32)
         normed_two = layer_norm(mixed, gains[1]).astype(jnp.bfloat16)
         flat = normed_two.reshape(n_rows * n_cols, width)

time: 1460 us -> 1420 us (0.973)
  local copies, waits for them, and re-layouts: 333 us -> 300 us
    convert_element_type x7 -> x5, local copies, waits for them, and re-layouts: 94 us -> 65.1 us  [run_block(): mixed = base + spectral.astype(jnp.float32)]
  transfers between devices with their start and end apart: 11 -> 11, of which waited for: 6 -> 6; matrix products, arithmetic and copies ran while one was open for 33% -> 32% of each run, Pallas kernels for 0% -> 0%
where the time goes in v1:
time: 1420 us; the launch traced here: 1410 us
  waiting for transfers between devices  503 us (35%)
  local copies, waits for them, and re-layouts  300 us (21%)
  matrix products  180 us (13%)
  blocking collectives  146 us (10%)
  other arithmetic  141 us (10%)
  loops' own time  78.3 us (6%)
  starting transfers between devices  39.3 us (3%)
  between operations  18.7 us (1%)
    all_to_all x2, waiting for transfers between devices, run_block(): lax.all_to_all(normed, 'lon', split_axis=2, concat_axis=1, tiled=True)  181 us
    all_to_all x1, waiting for transfers between devices, run_block(): lax.all_to_all(synthesis, 'lat', split_axis=0, concat_axis=2, tiled=True)  128 us
    ppermute x1, waiting for transfers between devices, passed_along(): lax.ppermute(value, axis, [(source, source + steps) for source in range(l...  115 us
    all_to_all x1, blocking collectives, run_block(): lax.all_to_all(spectrum, 'lat', split_axis=2, concat_axis=0, tiled=True)  80.9 us
    another operation x1, loops' own time, legendre_table(): lax.scan(advance, (jnp.zeros_like(start), jnp.zeros_like(start)), jnp.ara...  78.3 us
    all_to_all x2, waiting for transfers between devices, run_block(): lax.all_to_all(jnp.stack(jnp.split(spectral, lax.axis_size('lon'), axis=1...  77.9 us
    dot_general x2, matrix products, run_block(): jnp.dot(flat, lax.all_gather(weight_in, 'lat', axis=0, tiled=True), prefe...  73.3 us
    dynamic_slice x112, local copies, waits for them, and re-layouts, legendre_table(): lax.scan(advance, (jnp.zeros_like(start), jnp.zeros_like(start)), jnp.ara...  66 us
  transfers between devices with their start and end apart: 11, of which 6 were waited for; matrix products, arithmetic and copies ran while one was open for 32% of the time, Pallas kernels for 0%

profile of v1, /device:TPU:0, one launch (start us, length us, event | category | flops | bytes accessed | tf_op | source)
XLA Modules:
  0.0 1406.3 jit_solution(3135311183727737770)
XLA Ops:
  13.6 3.8 fusion.29
  21.4 7.0 multiply_convert_fusion.2
  28.3 12.0 copy.89
  40.3 5.6 all-to-all-start
  46.2 4.7 constant_dynamic-slice_fusion.3
  51.1 88.8 %all-to-all-done = bf16[28,90,1024]{1,0,2:T(8,128)(2,1)} async-done(((bf16[28,90,1024]{1,0,2:T(8,128)(2,1)}), bf16[28,90,1024]{1,0,2:T(8,128)(2,1)}, u32[]{:S(2)}, u32[]{:S(2)}) %all-to-all-start) | async-done | bytes 5160992 | tf_op jit(solution)/shard_map/all_to_all | solution.py:110
  139.9 14.5 %copy.90 = bf16[28,90,4,256]{3,1,2,0:T(8,128)(2,1)} copy(bf16[28,90,4,256]{1,0,3,2:T(8,128)(2,1)} %bitcast.10) | data formatting | bytes 10321920 | tf_op jit(solution)/shard_map/all_to_all | solution.py:110
  154.3 8.3 all_to_all.87
  162.6 6.3 fusion.72
  169.0 3.8 fusion.73
  173.1 4.4 copy.91
  177.4 6.0 all-to-all-start.1
  183.4 162.5 %while.20 = (s32[]{:T(128)}, f32[24,112]{1,0:T(8,128)S(1)}, f32[24,112]{1,0:T(8,128)S(1)}, f32[112,24,112]{2,1,0:T(8,128)S(1)}, s32[112]{0:T(128)S(1)}, /*index=...) while((s32[]{:T(128)}, f32[24,112]{1,0:T(8,128)S(1)}, ...), condition=%wide.region_3.4_spmd.clone.clone.clone, body=%wide.region_2.3_spmd.clone.clone.clone.sunk | while | flops 24742 | bytes 66539 | solution.py:48
  354.6 3.9 fusion.62
  359.4 5.2 convert_bitcast_fusion.3
  368.2 5.1 all-to-all-start.2
  373.7 4.7 constant_dynamic-slice_fusion.2
  379.7 127.7 %all-to-all-done.2 = bf16[112,2,24,256]{3,1,2,0:T(2,128)(2,1)S(1)} async-done(((bf16[112,2,24,256]{3,1,2,0:T(2,128)(2,1)}), bf16[112,2,24,256]{3,1,2,0:T(2,128)(2,1)S(1)}, u32[]{:S(2)}, u32[]{:S(2)}) %all-to-all-start.2) | async-done | bytes 2752544 | tf_op jit(solution)/shard_map/all_to_all | solution.py:126
  508.3 4.6 fusion.47
  518.6 5.3 all-to-all-start.3
  524.0 8.2 reshape.637
  532.2 54.0 %all-to-all-done.3 = bf16[4,28,90,256]{3,2,1,0:T(8,128)(2,1)} async-done(((bf16[4,28,90,256]{3,2,1,0:T(8,128)(2,1)}), bf16[4,28,90,256]{3,2,1,0:T(8,128)(2,1)}, u32[]{:S(2)}, u32[]{:S(2)}) %all-to-all-start.3) | async-done | bytes 5160992 | tf_op jit(solution)/shard_map/all_to_all | solution.py:131
  586.2 4.1 convert_bitcast_fusion.1
  590.3 12.1 copy.100
  602.3 13.5 reshape.639
  615.9 7.2 fusion.57
  623.2 8.0 multiply_reduce_fusion.2
  631.4 10.3 copy.129
  641.7 38.2 %fusion.16.clone.4 = bf16[2520,4096]{1,0:T(8,128)(2,1)} fusion(bf16[1,1,1024,4096]{3,2,1,0:T(8,128)(2,1)} %all-gather.9.cloned.1.call-done, f32[2520,1024]{1,0:T(8,128)} %bitcast.214, f32[2520,1024]{1,0:T(8,128)} %reshape.637, f32[1024]{0:T(1024)S(1)} %bitcast.234, f32[2520]{0:T(1024)S(1)} %rsqrt.37, f32[2520]{0:T(1024)S(1)} %div.110, ...), kind=kOutput, calls=%fused_computation.24.clone.clone.clone.1 | convolution fusion | flops 21247672320 | bytes 49704640 | tf_op jit(solution)/shard_map/dot_general | solution.py:139
  679.9 28.6 %fusion.34 = f32[2520,1024]{1,0:T(8,128)} fusion(bf16[1,1,1024,4096]{3,2,1,0:T(8,128)(2,1)} %all-gather.11.cloned.1.call-done, bf16[2520,4096]{1,0:T(8,128)(2,1)} %fusion.16.clone.4), kind=kOutput, calls=%fused_computation.58 | convolution fusion | flops 21139292160 | bytes 39354368 | tf_op jit(solution)/shard_map/dot_general | solution.py:145
  708.5 11.2 reshape.632
  719.7 12.8 add_convert_fusion.1
  732.4 5.8 collective-permute-start
  739.0 114.7 %collective-permute-done = bf16[28,90,1024]{2,1,0:T(8,128)(2,1)} collective-permute-done((bf16[28,90,1024]{2,1,0:T(8,128)(2,1)}, bf16[28,90,1024]{2,1,0:T(8,128)(2,1)}, u32[]{:S(2)}, u32[]{:S(2)}) %collective-permute-start) | collective-permute-done | bytes 5160992 | tf_op jit(solution)/shard_map/ppermute | solution.py:13
  853.8 4.6 fusion.27
  860.8 3.9 multiply_convert_fusion.1
  864.6 12.0 copy.103
  876.6 5.6 all-to-all-start.4
  883.0 92.4 %all-to-all-done.4 = bf16[28,90,1024]{1,0,2:T(8,128)(2,1)} async-done(((bf16[28,90,1024]{1,0,2:T(8,128)(2,1)}), bf16[28,90,1024]{1,0,2:T(8,128)(2,1)}, u32[]{:S(2)}, u32[]{:S(2)}) %all-to-all-start.4) | async-done | bytes 5160992 | tf_op jit(solution)/shard_map/all_to_all | solution.py:110
  975.4 14.6 %copy.104 = bf16[28,90,4,256]{3,1,2,0:T(8,128)(2,1)} copy(bf16[28,90,4,256]{1,0,3,2:T(8,128)(2,1)} %bitcast.45) | data formatting | bytes 10321920 | tf_op jit(solution)/shard_map/all_to_all | solution.py:110
  990.0 8.3 all_to_all.100
  998.4 6.3 fusion.74
  1004.7 3.8 fusion.75
  1011.6 80.9 %all_to_all.118 = bf16[28,2,96,256]{3,1,0,2:T(2,128)(2,1)S(1)} all-to-all(bf16[28,2,96,256]{3,1,0,2:T(2,128)(2,1)S(1)} %copy.105), channel_id=1, replica_groups=mesh['section'=2,'lat'=4,'lon'=4] {'lat'}, dimensions={2} | all-to-all | bytes 5505024 | tf_op jit(solution)/shard_map/all_to_all | solution.py:115
  1093.9 3.9 fusion.65
  1099.1 5.1 convert_bitcast_fusion.2
  1106.4 64.6 %all_to_all.119 = bf16[112,2,24,256]{3,1,2,0:T(2,128)(2,1)S(1)} all-to-all(bf16[112,2,24,256]{3,1,2,0:T(2,128)(2,1)S(1)} %copy.111), channel_id=1, replica_groups=mesh['section'=2,'lat'=4,'lon'=4] {'lat'}, dimensions={0} | all-to-all | bytes 5505024 | tf_op jit(solution)/shard_map/all_to_all | solution.py:126
  1172.0 4.6 fusion.48
  1182.4 5.1 all-to-all-start.7
  1188.1 11.1 reshape.631
  1199.2 13.7 reshape.636
  1212.9 13.0 add_convert_fusion.2
  1225.8 23.9 %all-to-all-done.7 = bf16[4,28,90,256]{3,2,1,0:T(8,128)(2,1)} async-done(((bf16[4,28,90,256]{3,2,1,0:T(8,128)(2,1)}), bf16[4,28,90,256]{3,2,1,0:T(8,128)(2,1)}, u32[]{:S(2)}, u32[]{:S(2)}) %all-to-all-start.7) | async-done | bytes 5160992 | tf_op jit(solution)/shard_map/all_to_all | solution.py:131
  1249.7 4.1 convert_bitcast_fusion
  1253.8 12.2 copy.114
  1266.1 13.6 reshape.640
  1279.7 7.5 fusion.157
  1287.1 8.2 multiply_reduce_fusion
  1295.4 8.5 multiply_convert_fusion
  1303.8 7.9 reshape.633
  1311.8 35.2 %fusion.24.clone.4 = bf16[2520,4096]{1,0:T(8,128)(2,1)} fusion(bf16[2520,1024]{1,0:T(8,128)(2,1)} %reshape.633, bf16[1,1,1024,4096]{3,2,1,0:T(8,128)(2,1)} %all-gather.13.cloned.1.call-done), kind=kOutput, calls=%fused_computation.32.clone.clone.clone.1 | convolution fusion | flops 21232189440 | bytes 34193408 | tf_op jit(solution)/shard_map/dot_general | solution.py:139
  1347.0 28.9 %fusion.30 = f32[2520,1024]{1,0:T(8,128)} fusion(bf16[1,1,1024,4096]{3,2,1,0:T(8,128)(2,1)} %all-gather.15.cloned.1.call-done, bf16[2520,4096]{1,0:T(8,128)(2,1)} %fusion.24.clone.4), kind=kOutput, calls=%fused_computation.55 | convolution fusion | flops 21139292160 | bytes 39354368 | tf_op jit(solution)/shard_map/dot_general | solution.py:145
  1375.8 10.8 reshape.634
  1386.7 12.8 fusion.38
  (684 shorter events, 131.6 us)
Async XLA Ops:
  7.2 5.5 copy-start
  11.1 6.2 copy-start.2
  13.6 7.2 copy-start.22
  40.3 99.5 %all-to-all-start = ((bf16[28,90,1024]{1,0,2:T(8,128)(2,1)}), bf16[28,90,1024]{1,0,2:T(8,128)(2,1)}, u32[]{:S(2)}, u32[]{:S(2)}) async-start(bf16[28,90,1024]{1,0,2:T(8,128)(2,1)} %copy.89), calls=%async_computation | async-start | bytes 16777216 | tf_op jit(solution)/shard_map/all_to_all | solution.py:110
  46.0 595.7 %all-gather.9.cloned.1.call-start = ((), (), s32[]{:S(2)}) async-start(), calls=%async_computation.8 | async-start | bytes 10485760 | tf_op jit(solution)/shard_map/all_gather | solution.py:141
  162.6 6.3 copy-start.4
  173.1 172.8 %copy-start.23 = (s32[2]{0:T(128)S(1)}, s32[2]{0:T(128)}, u32[]{:S(2)}) copy-start(s32[2]{0:T(128)} %param.18) | copy-start | bytes 28
  173.1 173.6 %copy-start.24 = (s32[2]{0:T(128)S(1)}, s32[2]{0:T(128)}, u32[]{:S(2)}) copy-start(s32[2]{0:T(128)} %param.17) | copy-start | bytes 28
  177.4 171.7 %copy-start.17 = (f32[1,2,2,112,256]{4,3,2,1,0:T(8,128)S(1)}, f32[1,2,2,112,256]{4,3,2,1,0:T(8,128)}, u32[]{:S(2)}) copy-start(f32[1,2,2,112,256]{4,3,2,1,0:T(8,128)} %param.21) | copy-start | bytes 1376260
  177.4 173.9 %all-to-all-start.1 = ((bf16[28,2,96,256]{3,1,0,2:T(2,128)(2,1)}), bf16[28,2,96,256]{3,1,0,2:T(2,128)(2,1)}, u32[]{:S(2)}, u32[]{:S(2)}) async-start(bf16[28,2,96,256]{3,1,0,2:T(2,128)(2,1)} %copy.91), calls=%async_computation.1 | async-start | bytes 5505024 | tf_op jit(solution)/shard_map/all_to_all | solution.py:115
  345.9 4.0 copy-start.10
  347.7 11.7 copy-start.6
  349.9 8.5 copy-start.18
  351.4 3.2 copy-start.8
  368.2 139.2 %all-to-all-start.2 = ((bf16[112,2,24,256]{3,1,2,0:T(2,128)(2,1)}), bf16[112,2,24,256]{3,1,2,0:T(2,128)(2,1)S(1)}, u32[]{:S(2)}, u32[]{:S(2)}) async-start(bf16[112,2,24,256]{3,1,2,0:T(2,128)(2,1)} %copy.97), calls=%async_computation.2 | async-start | bytes 5505024 | tf_op jit(solution)/shard_map/all_to_all | solution.py:126
  373.3 306.5 %all-gather.11.cloned.1.call-start = ((), (), s32[]{:S(2)}) async-start(), calls=%async_computation.9 | async-start | bytes 10485760 | tf_op jit(solution)/shard_map/all_gather | solution.py:147
  379.1 129.1 %copy-start.11 = (f32[1,96,360]{2,1,0:T(8,128)}, f32[1,96,360]{2,1,0:T(8,128)S(1)}, u32[]{:S(2)}) copy-start(f32[1,96,360]{2,1,0:T(8,128)S(1)} %cosine_multiply_fusion.1) | copy-start | bytes 414724
  379.7 128.5 %copy-start.13 = (f32[1,96,360]{2,1,0:T(8,128)}, f32[1,96,360]{2,1,0:T(8,128)S(1)}, u32[]{:S(2)}) copy-start(f32[1,96,360]{2,1,0:T(8,128)S(1)} %sine_multiply_fusion) | copy-start | bytes 414724
  518.6 67.6 %all-to-all-start.3 = ((bf16[4,28,90,256]{3,2,1,0:T(8,128)(2,1)}), bf16[4,28,90,256]{3,2,1,0:T(8,128)(2,1)}, u32[]{:S(2)}, u32[]{:S(2)}) async-start(bf16[4,28,90,256]{3,2,1,0:T(8,128)(2,1)} %pad_maximum_fusion), calls=%async_computation.3 | async-start | bytes 11010048 | tf_op jit(solution)/shard_map/all_to_all | solution.py:131
  732.4 121.3 %collective-permute-start = (bf16[28,90,1024]{2,1,0:T(8,128)(2,1)}, bf16[28,90,1024]{2,1,0:T(8,128)(2,1)}, u32[]{:S(2)}, u32[]{:S(2)}) collective-permute-start(bf16[28,90,1024]{2,1,0:T(8,128)(2,1)} %add_convert_fusion.1), channel_id=1, source_target_pairs={{0,16},{1,17},{2,18},{3,19},{4,20},{5,21},{6,22},{7,23},{8,24},{9,... | collective-permute-start | bytes 15482888 | tf_op jit(solution)/shard_map/ppermute | solution.py:13
  858.4 2.3 copy-start.3
  858.4 2.3 copy-start.21
  876.6 98.8 %all-to-all-start.4 = ((bf16[28,90,1024]{1,0,2:T(8,128)(2,1)}), bf16[28,90,1024]{1,0,2:T(8,128)(2,1)}, u32[]{:S(2)}, u32[]{:S(2)}) async-start(bf16[28,90,1024]{1,0,2:T(8,128)(2,1)} %copy.103), calls=%async_computation.4 | async-start | bytes 16777216 | tf_op jit(solution)/shard_map/all_to_all | solution.py:110
  882.3 429.5 %all-gather.13.cloned.1.call-start = ((), (), s32[]{:S(2)}) async-start(), calls=%async_computation.10 | async-start | bytes 10485760 | tf_op jit(solution)/shard_map/all_gather | solution.py:141
  998.3 6.3 copy-start.5
  1092.5 1.3 copy-start.9
  1093.5 4.3 copy-start.15
  1093.5 4.3 copy-start.16
  1093.5 4.3 copy-start.19
  1097.8 1.3 copy-start.7
  1171.0 0.9 copy-start.12
  1171.0 1.0 copy-start.14
  1182.4 67.4 %all-to-all-start.7 = ((bf16[4,28,90,256]{3,2,1,0:T(8,128)(2,1)}), bf16[4,28,90,256]{3,2,1,0:T(8,128)(2,1)}, u32[]{:S(2)}, u32[]{:S(2)}) async-start(bf16[4,28,90,256]{3,2,1,0:T(8,128)(2,1)} %pad_maximum_fusion.1), calls=%async_computation.7 | async-start | bytes 11010048 | tf_op jit(solution)/shard_map/all_to_all | solution.py:131
  1187.5 159.5 %all-gather.15.cloned.1.call-start = ((), (), s32[]{:S(2)}) async-start(), calls=%async_computation.11 | async-start | bytes 10485760 | tf_op jit(solution)/shard_map/all_gather | solution.py:147
  1279.7 15.7 %slice-start = ((s8[5505024]{0:T(1024)(128)(4,1)}), s8[4194304]{0:T(1024)(128)(4,1)S(1)}, s32[]{:S(2)}) async-start(s8[5505024]{0:T(1024)(128)(4,1)} %bitcast.201), calls=%async_computation.12 | async-start | bytes 8388608
  1287.1 8.2 slice-start.1
  1287.1 8.2 copy-start.20
  1386.7 12.8 copy-start.1
Sparse Core Ops, SparseCore 0:
  51.0 178.0 all-gather.8
  378.6 191.4 all-gather.10
  884.7 178.0 all-gather.12
  1189.6 149.1 all-gather.14
